TPU v7x, 8 devices: a whole 2x2x1 slice. The times are simulated.
8 devices in a mesh: rep: 1 (over z), fsdp: 8 (over y, x, core).
Axes of the slice: x: 2, y: 2, z: 1, core: 2. Of those that a mesh axis runs over, the one named last changes fastest.
Arguments:
- act_in: bfloat16 [12, 4096, 3072], P(None, ('rep', 'fsdp'))
- cot_out: bfloat16 [12, 4096, 3072], P(None, ('rep', 'fsdp'))
- lengths: int32 [12, 8], P(None, ('rep', 'fsdp'))
- w_in: bfloat16 [1, 3072, 8192], P(None, 'fsdp')
- w_out: bfloat16 [1, 8192, 3072], P(None, 'fsdp')
Outputs:
- output 1: float32 [1, 3072, 8192], P(None, ('rep', 'fsdp'))
- output 2: float32 [1, 8192, 3072], P(None, ('rep', 'fsdp'))
All inputs are finite; a program needn't handle non-finite values.
Results may differ from a plain program's by a relative error of at most 0.00939663.
Values are sent between devices in bfloat16 or wider.
A program may use at most 1 GiB of HBM per device.

v0:
```python
import functools
import math
import jax
import jax.numpy as jnp
from jax import lax
from jax.experimental import pallas as pl
from jax.experimental.pallas import tpu as pltpu
from jax.sharding import PartitionSpec as P


SQRT_HALF = math.sqrt(0.5)
INV_SQRT_TAU = 1.0 / math.sqrt(2.0 * math.pi)

CHUNKS = 4
GATHERS = ((0, 1), (1, 2), (2, 4))
BLOCK = 512
ALIGN = 16
VMEM_LIMIT = 66 * 1024 * 1024 - 2 * 1024 * 1024 - 65536


def pack_kernel(meta, in_ref, *refs, micro, tok, last_call):
    out, buf, sems = refs[-3:]
    k = pl.program_id(0)
    bits = [1 << b for b in range(tok.bit_length() - 1, ALIGN.bit_length() - 2, -1)]

    def segment(step, act):
        slot = lax.rem(step, 2)
        rows = jnp.bitwise_and(meta[step] + (ALIGN - 1), -ALIGN)
        offset = meta[micro + step]
        for bit in bits:
            @pl.when(jnp.bitwise_and(rows, bit) != 0)
            def _():
                first = pl.multiple_of(jnp.bitwise_and(rows, -2 * bit), ALIGN)
                dest = pl.multiple_of(offset + first, ALIGN)
                act(pltpu.make_async_copy(buf.at[slot, pl.ds(first, bit)], out.at[pl.ds(dest, bit)], sems.at[slot]))

    @pl.when(k >= 2)
    def _():
        segment(k - 2, lambda copy: copy.wait())

    slot = lax.rem(k, 2)
    buf[slot] = in_ref[0]
    length = meta[k]
    edge = pl.multiple_of(jnp.minimum(jnp.bitwise_and(length, -ALIGN), tok - ALIGN), ALIGN)
    row = edge + lax.broadcasted_iota(jnp.int32, (ALIGN, buf.shape[-1]), 0)
    kept = jnp.where(row < length, buf[slot, pl.ds(edge, ALIGN)].astype(jnp.float32), 0.0)
    buf[slot, pl.ds(edge, ALIGN)] = kept.astype(buf.dtype)
    segment(k, lambda copy: copy.start())

    @pl.when(k == micro - 1)
    def _():
        segment(k - 1, lambda copy: copy.wait())
        segment(k, lambda copy: copy.wait())
        if last_call:
            total, gap = meta[2 * micro], meta[2 * micro + 1]
            buf[0] = jnp.zeros(buf.shape[1:], buf.dtype)

            def tail(act):
                for bit in bits[1:]:
                    @pl.when(jnp.bitwise_and(gap, bit) != 0)
                    def _():
                        first = jnp.bitwise_and(gap, -2 * bit)
                        dest = pl.multiple_of(total + first, ALIGN)
                        act(pltpu.make_async_copy(buf.at[0, pl.ds(0, bit)], out.at[pl.ds(dest, bit)], sems.at[0]))

            tail(lambda copy: copy.start())
            tail(lambda copy: copy.wait())


def pack(meta, tokens, packed, cap):
    micro, tok, width = tokens.shape
    hbm = pl.BlockSpec(memory_space=pltpu.MemorySpace.HBM)
    given = () if packed is None else (packed,)
    return pl.pallas_call(
        functools.partial(pack_kernel, micro=micro, tok=tok, last_call=packed is not None),
        grid_spec=pltpu.PrefetchScalarGridSpec(
            num_scalar_prefetch=1,
            grid=(micro,),
            in_specs=[pl.BlockSpec((1, tok, width), lambda k, meta: (k, 0, 0))] + [hbm] * len(given),
            out_specs=hbm,
            scratch_shapes=[pltpu.VMEM((2, tok, width), tokens.dtype), pltpu.SemaphoreType.DMA((2,))],
        ),
        out_shape=jax.ShapeDtypeStruct((cap, width), tokens.dtype),
        input_output_aliases={} if packed is None else {2: 0},
        compiler_params=pltpu.CompilerParams(dimension_semantics=("arbitrary",), vmem_limit_bytes=32 * 1024 * 1024),
        cost_estimate=pl.CostEstimate(flops=15_000_000_000, bytes_accessed=4 * tokens.size, transcendentals=0),
        name="pack_own" if packed is None else "pack_partner",
    )(meta, tokens, *given)


def grads_kernel(meta, x_ref, e_ref, w1_hbm, w2_hbm, grads_hbm, w1, w2, acc_i, acc_o, act_t, dpre_t, sems, *, w1_at, w2_at):
    i = pl.program_id(0)
    hidden_size, width = w2.shape
    slab_width = w1_hbm.shape[-1]
    parts = acc_i.shape[0]
    part_width = width // parts
    piece = hidden_size // parts
    block = x_ref.shape[0]

    @pl.when(i == 0)
    def _():
        core = meta[1]
        copies = []
        for q in range(parts):
            for k in range(2):
                column = pl.multiple_of((2 * q + (core if k == 0 else 1 - core)) * slab_width, 128)
                source = w1_hbm.at[q, w1_at[0], pl.ds(w1_at[1] + k * hidden_size, hidden_size)]
                copies.append(pltpu.make_async_copy(source, w1.at[:, pl.ds(column, slab_width)], sems.at[0]))
            if w2_at is None:
                continue
            for k in range(width // slab_width):
                source = w2_hbm.at[q, w2_at[0], pl.ds(w2_at[1] + k * piece, piece)]
                copies.append(pltpu.make_async_copy(source, w2.at[pl.ds(q * piece, piece), pl.ds(k * slab_width, slab_width)], sems.at[1]))
        if w2_at is None:
            copies.append(pltpu.make_async_copy(w2_hbm, w2, sems.at[1]))
        for copy in copies:
            copy.start()
        acc_i[...] = jnp.zeros_like(acc_i)
        acc_o[...] = jnp.zeros_like(acc_o)
        for copy in copies:
            copy.wait()

    @pl.when(i < meta[0])
    def _():
        sub = 256
        transposed = (((1,), (1,)), ((), ()))

        def hidden(t, carry):
            rows = pl.ds(pl.multiple_of(t * sub, sub), sub)
            pre = lax.dot_general(w1[...], x_ref[rows, :], transposed, preferred_element_type=jnp.float32)
            d_act = lax.dot_general(w2[...], e_ref[rows, :], transposed, preferred_element_type=jnp.float32)
            z = pre.astype(jnp.bfloat16).astype(jnp.float32)
            cdf = 0.5 * (1.0 + lax.erf(z * SQRT_HALF))
            slope = cdf + z * jnp.exp(-0.5 * z * z) * INV_SQRT_TAU
            act_t[:, rows] = (z * cdf).astype(jnp.bfloat16)
            dpre_t[:, rows] = (d_act * slope).astype(jnp.bfloat16)
            return carry

        lax.fori_loop(0, block // sub, hidden, 0)

        def results(p):
            yield pltpu.make_async_copy(acc_i.at[p], grads_hbm.at[p, 0], sems.at[0])
            for q in range(parts):
                yield pltpu.make_async_copy(
                    acc_o.at[p, pl.ds(q * piece, piece)],
                    grads_hbm.at[q, 1, pl.ds(pl.multiple_of(p * piece, 8), piece)], sems.at[1])

        last = i == meta[0] - 1

        def accumulate(p, carry):
            columns = pl.ds(pl.multiple_of(p * part_width, 128), part_width)
            acc_o[p] += jnp.dot(act_t[...], e_ref[:, columns], preferred_element_type=jnp.float32)
            acc_i[p] += jnp.dot(dpre_t[...], x_ref[:, columns], preferred_element_type=jnp.float32)

            @pl.when(last)
            def _():
                for copy in results(p):
                    copy.start()

            return carry

        lax.fori_loop(0, parts, accumulate, 0)

        @pl.when(last)
        def _():
            for p in range(parts):
                for copy in results(p):
                    copy.wait()


def chunk_grads(meta, x_packed, e_packed, w1_from, w1_at, w2_from, w2_at, hidden):
    cap, width = x_packed.shape
    parts = w1_from.shape[0]
    hbm = pl.BlockSpec(memory_space=pltpu.MemorySpace.HBM)
    tokens = pl.BlockSpec((BLOCK, width), lambda i, meta: (jnp.minimum(i, meta[0] - 1), 0))
    return pl.pallas_call(
        functools.partial(grads_kernel, w1_at=w1_at, w2_at=w2_at),
        grid_spec=pltpu.PrefetchScalarGridSpec(
            num_scalar_prefetch=1,
            grid=(cap // BLOCK,),
            in_specs=[tokens, tokens, hbm, hbm],
            out_specs=hbm,
            scratch_shapes=[
                pltpu.VMEM((hidden, width), jnp.bfloat16),
                pltpu.VMEM((hidden, width), jnp.bfloat16),
                pltpu.VMEM((parts, hidden, width // parts), jnp.float32),
                pltpu.VMEM((parts, hidden, width // parts), jnp.float32),
                pltpu.VMEM((hidden, BLOCK), jnp.bfloat16),
                pltpu.VMEM((hidden, BLOCK), jnp.bfloat16),
                pltpu.SemaphoreType.DMA((2,)),
            ],
        ),
        out_shape=jax.ShapeDtypeStruct((parts, 2, hidden, width // parts), jnp.float32),
        compiler_params=pltpu.CompilerParams(dimension_semantics=("arbitrary",), vmem_limit_bytes=VMEM_LIMIT),
        cost_estimate=pl.CostEstimate(flops=8 * 7168 * width * hidden, bytes_accessed=8 * 7168 * width, transcendentals=0),
        name="chunk_grads",
    )(meta, x_packed, e_packed, w1_from, w2_from)


def turn_kernel(core, w_ref, out_ref):
    chunks, piece, _ = out_ref.shape
    for j in range(chunks):
        out_ref[j] = w_ref[:, j * piece:(j + 1) * piece].T


def turned_columns(core, w, other, chips):
    rows, full = w.shape
    per_device = full // (2 * chips)
    piece = per_device // CHUNKS
    return pl.pallas_call(
        turn_kernel,
        grid_spec=pltpu.PrefetchScalarGridSpec(
            num_scalar_prefetch=1,
            grid=(chips,),
            in_specs=[pl.BlockSpec((rows, per_device), lambda q, core: (0, 2 * q + jnp.bitwise_xor(core[0], other)))],
            out_specs=pl.BlockSpec((CHUNKS, piece, rows), lambda q, core: (0, q, 0)),
        ),
        out_shape=jax.ShapeDtypeStruct((CHUNKS, chips * piece, rows), w.dtype),
        compiler_params=pltpu.CompilerParams(dimension_semantics=("arbitrary",)),
        cost_estimate=pl.CostEstimate(flops=3_000_000_000, bytes_accessed=2 * w.size, transcendentals=0),
        name="turn_other" if other else "turn_own",
    )(core, w)


def place_kernel(core, kept_ref, got_ref, rows_ref, *refs):
    gi_ref, go_ref = refs[-2:]
    mine = pl.program_id(1) == core[0]

    @pl.when(mine)
    def _():
        gi_ref[...] = kept_ref[0].T

    @pl.when(jnp.logical_not(mine))
    def _():
        gi_ref[...] = got_ref[...].T

    go_ref[...] = rows_ref[0]


def place(core, reduced, got, outs, j, chips):
    _, hidden, part_width = reduced.shape
    piece = hidden // chips
    rows = part_width // 2
    given = () if outs is None else outs
    anywhere = pl.BlockSpec(memory_space=pltpu.MemorySpace.HBM)
    return pl.pallas_call(
        place_kernel,
        grid_spec=pltpu.PrefetchScalarGridSpec(
            num_scalar_prefetch=1,
            grid=(chips, 2),
            in_specs=[
                pl.BlockSpec((1, piece, rows), lambda q, c, core: (0, q, core[0])),
                pl.BlockSpec((piece, rows), lambda q, c, core: (q, 0)),
                pl.BlockSpec((1, piece, part_width), lambda q, c, core: (1, q, 0)),
            ] + [anywhere] * len(given),
            out_specs=[
                pl.BlockSpec((rows, piece), lambda q, c, core: (0, (2 * q + c) * CHUNKS + j)),
                pl.BlockSpec((piece, part_width), lambda q, c, core: (j, q)),
            ],
        ),
        out_shape=[
            jax.ShapeDtypeStruct((rows, 2 * CHUNKS * hidden), jnp.float32),
            jax.ShapeDtypeStruct((CHUNKS * piece, chips * part_width), jnp.float32),
        ],
        input_output_aliases={} if outs is None else {4: 0, 5: 1},
        compiler_params=pltpu.CompilerParams(dimension_semantics=("arbitrary", "arbitrary")),
        cost_estimate=pl.CostEstimate(flops=2_000_000_000, bytes_accessed=12 * reduced.size, transcendentals=0),
    )(core, reduced, got, reduced, *given)


def solution(mesh):
    shard_spec = P(None, ('rep', 'fsdp'), None)
    len_spec = P(None, ('rep', 'fsdp'))
    weight_spec = P(None, 'fsdp', None)
    count = mesh.shape['fsdp']
    chips = count // 2
    same_core = [[2 * q + c for q in range(chips)] for c in range(2)]
    swap = [(d, d ^ 1) for d in range(count)]

    def local_step(act_in, cot_out, lengths, w_in, w_out):
        micro, tok, width = act_in.shape
        core = lax.rem(lax.axis_index('fsdp'), 2)
        rows_in, rows_out = w_in.shape[1], w_out.shape[1]
        piece = rows_out // CHUNKS
        hidden = chips * piece

        lens = lengths[:, 0]
        lens_other = lax.ppermute(lens, 'fsdp', swap)
        x_sent, e_sent, lens_other = lax.optimization_barrier((act_in, cot_out, lens_other))
        x_other = lax.ppermute(x_sent, 'fsdp', swap)
        e_other = lax.ppermute(e_sent, 'fsdp', swap)

        core_ref = core.reshape(1).astype(jnp.int32)
        w_got = lax.ppermute(turned_columns(core_ref, w_in[0], 1, chips), 'fsdp', swap)
        w_mine = turned_columns(core_ref, w_in[0], 0, chips)

        def gather(slabs):
            shape = slabs.shape
            flat = slabs.reshape(-1, shape[-1])
            flat = lax.all_gather(flat, 'fsdp', axis=0, tiled=True, axis_index_groups=same_core)
            return flat.reshape(chips, *shape)

        def out_rows(first, last):
            rows = w_out[0, first * piece:last * piece].reshape(last - first, piece, width // rows_in, rows_in)
            return rows.transpose(0, 2, 1, 3).reshape(last - first, -1, rows_in)

        weights = []
        for first, last in GATHERS:
            if first == 0:
                w2 = lax.all_gather(w_out[0, :piece], 'fsdp', axis=0, tiled=True, axis_index_groups=same_core)
                w1 = gather(jnp.concatenate([w_mine[:1], w_got[:1]], axis=1))
                weights.append((w1, (0, 0), w2, None))
            else:
                both = gather(jnp.concatenate([w_mine[first:last], w_got[first:last], out_rows(first, last)], axis=1))
                weights += [(both, (n, 0), both, (n, 2 * hidden)) for n in range(last - first)]

        def rounded(n):
            return (n + (ALIGN - 1)) // ALIGN * ALIGN

        cap = 2 * micro * tok
        ends = jnp.cumsum(rounded(lens))
        meta_own = jnp.concatenate([lens, ends - rounded(lens)])
        x_packed, e_packed = (pack(meta_own, tokens, None, cap) for tokens in (act_in, cot_out))
        ends_other = ends[-1] + jnp.cumsum(rounded(lens_other))
        total = ends_other[-1]
        blocks = (total + BLOCK - 1) // BLOCK
        edge = jnp.stack([total, blocks * BLOCK - total])
        meta_other = jnp.concatenate([lens_other, ends_other - rounded(lens_other), edge])
        x_packed = pack(meta_other, x_other, x_packed, cap)
        e_packed = pack(meta_other, e_other, e_packed, cap)
        meta = jnp.stack([blocks, core]).astype(jnp.int32)

        outs = None
        for j in range(CHUNKS):
            part = chunk_grads(meta, x_packed, e_packed, *weights[j], hidden)
            part = part.reshape(-1, part.shape[-1])
            reduced = lax.psum_scatter(part, 'fsdp', scatter_dimension=0, tiled=True, axis_index_groups=same_core)
            reduced = reduced.reshape(2, hidden, -1)
            away = lax.dynamic_slice_in_dim(reduced[0], (1 - core) * rows_in, rows_in, axis=1)
            got = lax.ppermute(away, 'fsdp', swap)
            outs = place(core_ref, reduced, got, outs, j, chips)
        return outs[0][None], outs[1][None]

    return jax.shard_map(local_step, mesh=mesh, in_specs=(shard_spec, shard_spec, len_spec, weight_spec, weight_spec), out_specs=(shard_spec, shard_spec), check_vma=False)
```

profile of v0, /device:TPU:0, one launch (start us, length us, event | category | flops | bytes accessed | tf_op | source)
XLA Modules:
  0.0 1412.7 jit_solution(3988170484943243299)
XLA Ops:
  7.2 3.2 fusion.2
  10.5 4.6 turn_other.1
  16.0 4.8 turn_own.1
  20.8 1.6 fusion.3
  22.4 1.5 fusion.4
  23.9 1.3 pad_maximum_fusion.2
  27.4 1.9 pad_maximum_fusion.1
  29.8 1.9 slice-done.4
  33.3 1.7 slice.70
  35.1 2.9 pad_maximum_fusion
  39.2 23.0 %pack_own.3.refs_0_ = bf16[12288,3072]{1,0:T(8,128)(2,1)} custom-call(s32[24]{0:T(128)S(1)} %pad_add_fusion.2.meta, bf16[12,512,3072]{2,1,0:T(8,128)(2,1)} %in_ref.3), custom_call_target="tpu_custom_call" | custom-call | flops 15000000512 | bytes 75497472 | tf_op jit(solution)/shard_map/pack_own/pallas_call | solution.py:74
  62.2 24.2 %pack_own.2.refs_0_ = bf16[12288,3072]{1,0:T(8,128)(2,1)} custom-call(s32[24]{0:T(128)S(1)} %pad_add_fusion.2.meta, bf16[12,512,3072]{2,1,0:T(8,128)(2,1)} %in_ref.2), custom_call_target="tpu_custom_call" | custom-call | flops 15000000512 | bytes 75497472 | tf_op jit(solution)/shard_map/pack_own/pallas_call | solution.py:74
  90.6 24.8 %pack_partner.3.e_ref = bf16[12288,3072]{1,0:T(8,128)(2,1)} custom-call(s32[26]{0:T(128)S(1)} %pad_add_fusion.1.meta, bf16[12,512,3072]{2,1,0:T(8,128)(2,1)} %collective-permute-done.2.in_ref, bf16[12288,3072]{1,0:T(8,128)(2,1)} %pack_own.3.refs_0_), custom_call_target="tpu_custom_call", output_to_operand_aliasing={{}: (2, {})} | custom-call | flops 15000000512 | bytes 75497472 | tf_op jit(solution)/shard_map/pack_partner/pallas_call | solution.py:74
  115.4 20.7 %collective-permute-done.1.in_ref = bf16[12,512,3072]{2,1,0:T(8,128)(2,1)} collective-permute-done((bf16[12,512,3072]{2,1,0:T(8,128)(2,1)}, bf16[12,512,3072]{2,1,0:T(8,128)(2,1)}, u32[]{:S(2)}, u32[]{:S(2)}) %collective-permute-start.1) | collective-permute-done | bytes 37748768 | tf_op jit(solution)/shard_map/ppermute | solution.py:290
  136.0 25.4 %pack_partner.2.x_ref = bf16[12288,3072]{1,0:T(8,128)(2,1)} custom-call(s32[26]{0:T(128)S(1)} %pad_add_fusion.1.meta, bf16[12,512,3072]{2,1,0:T(8,128)(2,1)} %collective-permute-done.1.in_ref, bf16[12288,3072]{1,0:T(8,128)(2,1)} %pack_own.2.refs_0_), custom_call_target="tpu_custom_call", output_to_operand_aliasing={{}: (2, {})} | custom-call | flops 15000000512 | bytes 75497472 | tf_op jit(solution)/shard_map/pack_partner/pallas_call | solution.py:74
  161.5 233.2 %chunk_grads.7 = f32[4,2,1024,768]{3,2,1,0:T(8,128)} custom-call(s32[2]{0:T(128)} %pad_add_fusion.meta, bf16[12288,3072]{1,0:T(8,128)(2,1)} %pack_partner.2.x_ref, bf16[12288,3072]{1,0:T(8,128)(2,1)} %pack_partner.3.e_ref, bf16[4,1,2048,384]{3,2,1,0:T(8,128)(2,1)} %bitcast.78, bf16[1024,3072]{1,0:T(8,128)(2,1)} %bitcast.77), custom_call_target="tpu_custom_call" | custom-call | flops 180388626432 | bytes 176160768 | tf_op jit(solution)/shard_map/chunk_grads/pallas_call | solution.py:176
  395.1 233.1 %chunk_grads.6 = f32[4,2,1024,768]{3,2,1,0:T(8,128)} custom-call(s32[2]{0:T(128)} %pad_add_fusion.meta, bf16[12288,3072]{1,0:T(8,128)(2,1)} %pack_partner.2.x_ref, bf16[12288,3072]{1,0:T(8,128)(2,1)} %pack_partner.3.e_ref, bf16[4,1,4096,384]{3,2,1,0:T(8,128)(2,1)} %bitcast.73, bf16[4,1,4096,384]{3,2,1,0:T(8,128)(2,1)} %bitcast.74), custom_call_target="tpu_custom_call" | custom-call | flops 180388626432 | bytes 176160768 | tf_op jit(solution)/shard_map/chunk_grads/pallas_call | solution.py:176
  628.6 234.3 %chunk_grads.5 = f32[4,2,1024,768]{3,2,1,0:T(8,128)} custom-call(s32[2]{0:T(128)} %pad_add_fusion.meta, bf16[12288,3072]{1,0:T(8,128)(2,1)} %pack_partner.2.x_ref, bf16[12288,3072]{1,0:T(8,128)(2,1)} %pack_partner.3.e_ref, bf16[4,2,4096,384]{3,2,1,0:T(8,128)(2,1)} %bitcast.69, bf16[4,2,4096,384]{3,2,1,0:T(8,128)(2,1)} %bitcast.70), custom_call_target="tpu_custom_call" | custom-call | flops 180388626432 | bytes 176160768 | tf_op jit(solution)/shard_map/chunk_grads/pallas_call | solution.py:176
  863.3 234.0 %chunk_grads.4 = f32[4,2,1024,768]{3,2,1,0:T(8,128)} custom-call(s32[2]{0:T(128)} %pad_add_fusion.meta, bf16[12288,3072]{1,0:T(8,128)(2,1)} %pack_partner.2.x_ref, bf16[12288,3072]{1,0:T(8,128)(2,1)} %pack_partner.3.e_ref, bf16[4,2,4096,384]{3,2,1,0:T(8,128)(2,1)} %bitcast.71, bf16[4,2,4096,384]{3,2,1,0:T(8,128)(2,1)} %bitcast.72), custom_call_target="tpu_custom_call" | custom-call | flops 180388626432 | bytes 176160768 | tf_op jit(solution)/shard_map/chunk_grads/pallas_call | solution.py:176
  1097.4 2.3 slice-done
  1101.1 2.2 slice-done.1
  1103.3 1.4 constant_dynamic-slice_fusion.1
  1104.9 39.6 %reduce-scatter.7.cloned.1.call-done = f32[2048,768]{1,0:T(8,128)} async-done(((f32[8192,768]{1,0:T(8,128)}), f32[2048,768]{1,0:T(8,128)}) %reduce-scatter.7.cloned.1.call-update) | async-done | bytes 6291472 | tf_op jit(solution)/shard_map/reduce_scatter | solution.py:337
  1144.5 1.9 slice-done.2
  1146.4 1.3 constant_dynamic-slice_fusion.2
  1147.7 216.1 %reduce-scatter.5.cloned.1.call-done = f32[2048,768]{1,0:T(8,128)} async-done(((f32[8192,768]{1,0:T(8,128)}), f32[2048,768]{1,0:T(8,128)}) %reduce-scatter.5.cloned.1.call-update) | async-done | bytes 6291472 | tf_op jit(solution)/shard_map/reduce_scatter | solution.py:337
  1363.8 1.9 slice-done.3
  1365.6 1.3 constant_dynamic-slice_fusion.3
  1366.9 9.4 shard_map.68
  1376.4 9.4 shard_map.69
  1385.8 9.4 shard_map.70
  1396.4 9.4 shard_map.71
  (66 shorter events, 13.1 us)
Async XLA Ops:
  7.2 154.3 %all-gather.14.cloned.1.call-start = ((), (), s32[]{:S(2)}) async-start(), calls=%async_computation.11 | async-start | bytes 7864320 | tf_op jit(solution)/shard_map/all_gather | solution.py:310
  10.5 151.1 %all-gather.12.cloned.1.call-start = ((), (), s32[]{:S(2)}) async-start(), calls=%async_computation.10 | async-start | bytes 7864320 | tf_op jit(solution)/shard_map/all_gather | solution.py:300
  15.1 7.3 collective-permute-start.3
  23.9 1.4 copy-start.1
  25.3 369.8 %all-gather.10.cloned.1.call-start = ((), (), s32[]{:S(2)}) async-start(), calls=%async_computation.9 | async-start | bytes 15728640 | tf_op jit(solution)/shard_map/all_gather | solution.py:300
  25.4 1.2 collective-permute-start
  26.6 64.0 %collective-permute-start.2 = (bf16[12,512,3072]{2,1,0:T(8,128)(2,1)}, bf16[12,512,3072]{2,1,0:T(8,128)(2,1)}, u32[]{:S(2)}, u32[]{:S(2)}) collective-permute-start(bf16[12,512,3072]{2,1,0:T(8,128)(2,1)} %in_ref.3), channel_id=1, source_target_pairs={{0,1},{1,0},{2,3},{3,2},{4,5},{5,4},{6,7},{7,6}} | collective-permute-start | bytes 113246216 | tf_op jit(solution)/shard_map/ppermute | solution.py:291
  29.4 599.3 %all-gather.8.cloned.1.call-start = ((), (), s32[]{:S(2)}) async-start(), calls=%async_computation.4 | async-start | bytes 31457280 | tf_op jit(solution)/shard_map/all_gather | solution.py:300
  29.4 106.6 %collective-permute-start.1 = (bf16[12,512,3072]{2,1,0:T(8,128)(2,1)}, bf16[12,512,3072]{2,1,0:T(8,128)(2,1)}, u32[]{:S(2)}, u32[]{:S(2)}) collective-permute-start(bf16[12,512,3072]{2,1,0:T(8,128)(2,1)} %in_ref.2), channel_id=1, source_target_pairs={{0,1},{1,0},{2,3},{3,2},{4,5},{5,4},{6,7},{7,6}} | collective-permute-start | bytes 113246216 | tf_op jit(solution)/shard_map/ppermute | solution.py:290
  29.8 1.9 slice-start.4
  33.2 1.9 slice-start.5
  38.1 1059.3 %reduce-scatter.11.cloned.1.call-start = ((), (), s32[]{:S(2)}) async-start(), calls=%async_computation.8 | async-start | bytes 31457280 | tf_op jit(solution)/shard_map/reduce_scatter | solution.py:337
  394.8 706.3 %reduce-scatter.9.cloned.1.call-start = ((), (), s32[]{:S(2)}) async-start(), calls=%async_computation.7 | async-start | bytes 31457280 | tf_op jit(solution)/shard_map/reduce_scatter | solution.py:337
  628.3 516.2 %reduce-scatter.7.cloned.1.call-start = ((), (), s32[]{:S(2)}) async-start(), calls=%async_computation.6 | async-start | bytes 31457280 | tf_op jit(solution)/shard_map/reduce_scatter | solution.py:337
  862.9 500.8 %reduce-scatter.5.cloned.1.call-start = ((), (), s32[]{:S(2)}) async-start(), calls=%async_computation.5 | async-start | bytes 31457280 | tf_op jit(solution)/shard_map/reduce_scatter | solution.py:337
  1097.4 2.3 slice-start
  1100.9 266.0 %collective-permute-start.7 = (f32[1024,384]{1,0:T(8,128)}, f32[1024,384]{1,0:T(8,128)}, u32[]{:S(2)}, u32[]{:S(2)}) collective-permute-start(f32[1024,384]{1,0:T(8,128)} %constant_dynamic-slice_fusion), channel_id=1, source_target_pairs={{0,1},{1,0},{2,3},{3,2},{4,5},{5,4},{6,7},{7,6}} | collective-permute-start | bytes 4718600 | tf_op jit(solution)/shard_map/ppermute | solution.py:340
  1101.1 2.2 slice-start.1
  1104.7 271.7 %collective-permute-start.6 = (f32[1024,384]{1,0:T(8,128)}, f32[1024,384]{1,0:T(8,128)}, u32[]{:S(2)}, u32[]{:S(2)}) collective-permute-start(f32[1024,384]{1,0:T(8,128)} %constant_dynamic-slice_fusion.1), channel_id=1, source_target_pairs={{0,1},{1,0},{2,3},{3,2},{4,5},{5,4},{6,7},{7,6}} | collective-permute-start | bytes 4718600 | tf_op jit(solution)/shard_map/ppermute | solution.py:340
  1144.5 1.9 slice-start.2
  1147.7 238.1 %collective-permute-start.5 = (f32[1024,384]{1,0:T(8,128)}, f32[1024,384]{1,0:T(8,128)}, u32[]{:S(2)}, u32[]{:S(2)}) collective-permute-start(f32[1024,384]{1,0:T(8,128)} %constant_dynamic-slice_fusion.2), channel_id=1, source_target_pairs={{0,1},{1,0},{2,3},{3,2},{4,5},{5,4},{6,7},{7,6}} | collective-permute-start | bytes 4718600 | tf_op jit(solution)/shard_map/ppermute | solution.py:340
  1363.8 1.9 slice-start.3
  1366.9 28.3 %collective-permute-start.4 = (f32[1024,384]{1,0:T(8,128)}, f32[1024,384]{1,0:T(8,128)S(1)}, u32[]{:S(2)}, u32[]{:S(2)}) collective-permute-start(f32[1024,384]{1,0:T(8,128)} %constant_dynamic-slice_fusion.3), channel_id=1, source_target_pairs={{0,1},{1,0},{2,3},{3,2},{4,5},{5,4},{6,7},{7,6}} | collective-permute-start | bytes 4718600 | tf_op jit(solution)/shard_map/ppermute | solution.py:340
  1395.2 1.2 copy-start
Sparse Core Ops, SparseCore 0:
  10.6 67.2 all-gather.13
  79.7 64.4 all-gather.11
  146.0 116.8 all-gather.9
  265.0 222.0 all-gather.7
  490.0 216.1 reduce-scatter.10
  709.1 216.1 reduce-scatter.8
  928.3 216.1 reduce-scatter.6
  1147.6 216.1 reduce-scatter.4
where the time goes:
time: 1410 us
  Pallas kernels  1080 us (77%)
  waiting for transfers between devices  278 us (20%)
  local copies, waits for them, and re-layouts  28 us (2%)
  between operations  15.7 us (1%)
    pallas_call x4, Pallas kernels, chunk_grads(): pl.pallas_call(functools.partial(grads_kernel, w1_at=w1_at, w2_at=w2_at),...  935 us
    reduce_scatter x4, waiting for transfers between devices, local_step(): lax.psum_scatter(part, 'fsdp', scatter_dimension=0, tiled=True, axis_inde...  256 us
    pallas_call x4, Pallas kernels, pack(): pl.pallas_call(functools.partial(pack_kernel, micro=micro, tok=tok, last_...  97.4 us
    pallas_call x4, Pallas kernels, place(): pl.pallas_call(place_kernel, grid_spec=pltpu.PrefetchScalarGridSpec(num_s...  37.7 us
  transfers between devices with their start and end apart: 16, of which 4 were waited for; matrix products, arithmetic and copies ran while one was open for 2% of the time, Pallas kernels for 76%

commit v1 on v0

--- a/solution.py
+++ b/solution.py
@@ -88,7 +88,9 @@
     )(meta, tokens, *given)
 
 
-def grads_kernel(meta, x_ref, e_ref, w1_hbm, w2_hbm, grads_hbm, w1, w2, acc_i, acc_o, act_t, dpre_t, sems, *, w1_at, w2_at):
+def grads_kernel(meta, x_ref, e_ref, w1_hbm, w2_hbm, *refs, w1_at, w2_at):
+    *outs, w1, w2, acc_i, acc_o, act_t, dpre_t, sems = refs
+    grads_hbm = outs[0]
     i = pl.program_id(0)
     hidden_size, width = w2.shape
     slab_width = w1_hbm.shape[-1]
@@ -139,6 +141,18 @@
         lax.fori_loop(0, block // sub, hidden, 0)
 
         def results(p):
+            if len(outs) == 2:
+                half = part_width // 2
+                for rows, dest in ((meta[1], grads_hbm.at[p, pl.ds(0, hidden_size)]), (1 - meta[1], outs[1].at[p])):
+                    columns = pl.ds(pl.multiple_of(rows * half, 128), half)
+                    yield pltpu.make_async_copy(acc_i.at[p, :, columns], dest, sems.at[0])
+                for q in range(parts):
+                    for h in range(2):
+                        first = pl.multiple_of(2 * hidden_size + (2 * p + h) * piece, 8)
+                        yield pltpu.make_async_copy(
+                            acc_o.at[p, pl.ds(q * piece, piece), pl.ds(h * half, half)],
+                            grads_hbm.at[q, pl.ds(first, piece)], sems.at[1])
+                return
             yield pltpu.make_async_copy(acc_i.at[p], grads_hbm.at[p, 0], sems.at[0])
             for q in range(parts):
                 yield pltpu.make_async_copy(
@@ -168,18 +182,23 @@
                     copy.wait()
 
 
-def chunk_grads(meta, x_packed, e_packed, w1_from, w1_at, w2_from, w2_at, hidden):
+def chunk_grads(meta, x_packed, e_packed, w1_from, w1_at, w2_from, w2_at, hidden, halves):
     cap, width = x_packed.shape
     parts = w1_from.shape[0]
     hbm = pl.BlockSpec(memory_space=pltpu.MemorySpace.HBM)
     tokens = pl.BlockSpec((BLOCK, width), lambda i, meta: (jnp.minimum(i, meta[0] - 1), 0))
+    part_width = width // parts
+    if halves:
+        shapes = [(parts, 4 * hidden, part_width // 2), (parts, hidden, part_width // 2)]
+    else:
+        shapes = [(parts, 2, hidden, part_width)]
     return pl.pallas_call(
         functools.partial(grads_kernel, w1_at=w1_at, w2_at=w2_at),
         grid_spec=pltpu.PrefetchScalarGridSpec(
             num_scalar_prefetch=1,
             grid=(cap // BLOCK,),
             in_specs=[tokens, tokens, hbm, hbm],
-            out_specs=hbm,
+            out_specs=[hbm] * len(shapes),
             scratch_shapes=[
                 pltpu.VMEM((hidden, width), jnp.bfloat16),
                 pltpu.VMEM((hidden, width), jnp.bfloat16),
@@ -190,7 +209,7 @@
                 pltpu.SemaphoreType.DMA((2,)),
             ],
         ),
-        out_shape=jax.ShapeDtypeStruct((parts, 2, hidden, width // parts), jnp.float32),
+        out_shape=[jax.ShapeDtypeStruct(shape, jnp.float32) for shape in shapes],
         compiler_params=pltpu.CompilerParams(dimension_semantics=("arbitrary",), vmem_limit_bytes=VMEM_LIMIT),
         cost_estimate=pl.CostEstimate(flops=8 * 7168 * width * hidden, bytes_accessed=8 * 7168 * width, transcendentals=0),
         name="chunk_grads",
@@ -268,6 +287,56 @@
     )(core, reduced, got, reduced, *given)
 
 
+def place_last_kernel(core, reduced, gi_in, go_in, gi, go, buf, turned, in_sems, out_sems, *, j):
+    del gi_in, go_in
+    blocks, piece, half = buf.shape
+    chips = blocks // 4
+    loads = [pltpu.make_async_copy(reduced.at[pl.ds(b * piece, piece)], buf.at[b], in_sems.at[b]) for b in range(blocks)]
+    for load in loads:
+        load.start()
+    stores = []
+    for b in range(2 * chips):
+        side = core[0] if b < chips else 1 - core[0]
+        column = pl.multiple_of(((2 * (b % chips) + side) * CHUNKS + j) * piece, 128)
+        loads[b].wait()
+        turned[b] = buf[b].T
+        stores.append(pltpu.make_async_copy(turned.at[b], gi.at[:, pl.ds(column, piece)], out_sems.at[b]))
+        stores[-1].start()
+    for b in range(2 * chips, blocks):
+        loads[b].wait()
+        dest = go.at[pl.ds(j * piece, piece), pl.ds((b - 2 * chips) * half, half)]
+        stores.append(pltpu.make_async_copy(buf.at[b], dest, out_sems.at[b]))
+        stores[-1].start()
+    for store in stores:
+        store.wait()
+
+
+def place_last(core, reduced, outs, j, chips):
+    rows, half = reduced.shape
+    blocks = 4 * chips
+    piece = rows // blocks
+    anywhere = pl.BlockSpec(memory_space=pltpu.MemorySpace.HBM)
+    return pl.pallas_call(
+        functools.partial(place_last_kernel, j=j),
+        grid_spec=pltpu.PrefetchScalarGridSpec(
+            num_scalar_prefetch=1,
+            grid=(),
+            in_specs=[anywhere] * 3,
+            out_specs=[anywhere] * 2,
+            scratch_shapes=[
+                pltpu.VMEM((blocks, piece, half), jnp.float32),
+                pltpu.VMEM((2 * chips, half, piece), jnp.float32),
+                pltpu.SemaphoreType.DMA((blocks,)),
+                pltpu.SemaphoreType.DMA((blocks,)),
+            ],
+        ),
+        out_shape=[jax.ShapeDtypeStruct(out.shape, out.dtype) for out in outs],
+        input_output_aliases={2: 0, 3: 1},
+        compiler_params=pltpu.CompilerParams(vmem_limit_bytes=VMEM_LIMIT),
+        cost_estimate=pl.CostEstimate(flops=2_000_000_000, bytes_accessed=8 * reduced.size, transcendentals=0),
+    )(core, reduced, *outs)
+
+
 def solution(mesh):
     shard_spec = P(None, ('rep', 'fsdp'), None)
     len_spec = P(None, ('rep', 'fsdp'))
@@ -332,9 +401,15 @@
 
         outs = None
         for j in range(CHUNKS):
-            part = chunk_grads(meta, x_packed, e_packed, *weights[j], hidden)
+            halves = j == CHUNKS - 1
+            part, *away = chunk_grads(meta, x_packed, e_packed, *weights[j], hidden, halves)
+            if halves:
+                part = lax.dynamic_update_slice_in_dim(part, lax.ppermute(away[0], 'fsdp', swap), hidden, axis=1)
             part = part.reshape(-1, part.shape[-1])
             reduced = lax.psum_scatter(part, 'fsdp', scatter_dimension=0, tiled=True, axis_index_groups=same_core)
+            if halves:
+                outs = place_last(core_ref, reduced, outs, j, chips)
+                break
             reduced = reduced.reshape(2, hidden, -1)
             away = lax.dynamic_slice_in_dim(reduced[0], (1 - core) * rows_in, rows_in, axis=1)
             got = lax.ppermute(away, 'fsdp', swap)

time: 1410 us -> 1380 us (0.979)
  waiting for transfers between devices: 278 us -> 243 us
    reduce_scatter x4, waiting for transfers between devices: 256 us -> 212 us  [local_step(): lax.psum_scatter(part, 'fsdp', scatter_dimension=0, tiled=True, axis_inde...]
    pallas_call x4 -> x3, Pallas kernels: 37.7 us -> 28.7 us  [place(): pl.pallas_call(place_kernel, grid_spec=pltpu.PrefetchScalarGridSpec(num_s...]
  transfers between devices with their start and end apart: 16 -> 16, of which waited for: 4 -> 5; matrix products, arithmetic and copies ran while one was open for 2% -> 2% of each run, Pallas kernels for 76% -> 78%
where the time goes in v1:
time: 1380 us
  Pallas kernels  1080 us (78%)
  waiting for transfers between devices  243 us (18%)
  local copies, waits for them, and re-layouts  28.7 us (2%)
  between operations  15.7 us (1%)
    pallas_call x4, Pallas kernels, chunk_grads(): pl.pallas_call(functools.partial(grads_kernel, w1_at=w1_at, w2_at=w2_at),...  935 us
    reduce_scatter x4, waiting for transfers between devices, local_step(): lax.psum_scatter(part, 'fsdp', scatter_dimension=0, tiled=True, axis_inde...  212 us
    pallas_call x4, Pallas kernels, pack(): pl.pallas_call(functools.partial(pack_kernel, micro=micro, tok=tok, last_...  99.1 us
    pallas_call x3, Pallas kernels, place(): pl.pallas_call(place_kernel, grid_spec=pltpu.PrefetchScalarGridSpec(num_s...  28.7 us
  transfers between devices with their start and end apart: 16, of which 5 were waited for; matrix products, arithmetic and copies ran while one was open for 2% of the time, Pallas kernels for 78%

profile of v1, /device:TPU:0, one launch (start us, length us, event | category | flops | bytes accessed | tf_op | source)
XLA Modules:
  0.0 1376.6 jit_solution(11733893347521216831)
XLA Ops:
  7.2 3.7 fusion.2
  11.0 4.6 turn_other.1
  16.5 4.8 turn_own.1
  21.3 2.5 fusion.3
  25.0 1.3 pad_maximum_fusion.2
  27.7 1.7 copy.20
  29.8 1.9 pad_maximum_fusion.1
  32.2 1.4 slice-done.3
  36.6 2.9 pad_maximum_fusion
  40.7 23.8 %pack_own.3.refs_0_ = bf16[12288,3072]{1,0:T(8,128)(2,1)} custom-call(s32[24]{0:T(128)S(1)} %pad_add_fusion.2.meta, bf16[12,512,3072]{2,1,0:T(8,128)(2,1)} %in_ref.3), custom_call_target="tpu_custom_call" | custom-call | flops 15000000512 | bytes 75497472 | tf_op jit(solution)/shard_map/pack_own/pallas_call | solution.py:74
  64.5 24.5 %pack_own.2.refs_0_ = bf16[12288,3072]{1,0:T(8,128)(2,1)} custom-call(s32[24]{0:T(128)S(1)} %pad_add_fusion.2.meta, bf16[12,512,3072]{2,1,0:T(8,128)(2,1)} %in_ref.2), custom_call_target="tpu_custom_call" | custom-call | flops 15000000512 | bytes 75497472 | tf_op jit(solution)/shard_map/pack_own/pallas_call | solution.py:74
  93.1 25.1 %pack_partner.3.e_ref = bf16[12288,3072]{1,0:T(8,128)(2,1)} custom-call(s32[26]{0:T(128)S(1)} %pad_add_fusion.1.meta, bf16[12,512,3072]{2,1,0:T(8,128)(2,1)} %collective-permute-done.2.in_ref, bf16[12288,3072]{1,0:T(8,128)(2,1)} %pack_own.3.refs_0_), custom_call_target="tpu_custom_call", output_to_operand_aliasing={{}: (2, {})} | custom-call | flops 15000000512 | bytes 75497472 | tf_op jit(solution)/shard_map/pack_partner/pallas_call | solution.py:74
  118.2 18.8 %collective-permute-done.1.in_ref = bf16[12,512,3072]{2,1,0:T(8,128)(2,1)} collective-permute-done((bf16[12,512,3072]{2,1,0:T(8,128)(2,1)}, bf16[12,512,3072]{2,1,0:T(8,128)(2,1)}, u32[]{:S(2)}, u32[]{:S(2)}) %collective-permute-start.1) | collective-permute-done | bytes 37748768 | tf_op jit(solution)/shard_map/ppermute | solution.py:359
  137.0 25.7 %pack_partner.2.x_ref = bf16[12288,3072]{1,0:T(8,128)(2,1)} custom-call(s32[26]{0:T(128)S(1)} %pad_add_fusion.1.meta, bf16[12,512,3072]{2,1,0:T(8,128)(2,1)} %collective-permute-done.1.in_ref, bf16[12288,3072]{1,0:T(8,128)(2,1)} %pack_own.2.refs_0_), custom_call_target="tpu_custom_call", output_to_operand_aliasing={{}: (2, {})} | custom-call | flops 15000000512 | bytes 75497472 | tf_op jit(solution)/shard_map/pack_partner/pallas_call | solution.py:74
  162.8 233.2 %chunk_grads.7 = f32[4,2,1024,768]{3,2,1,0:T(8,128)} custom-call(s32[2]{0:T(128)} %pad_add_fusion.meta, bf16[12288,3072]{1,0:T(8,128)(2,1)} %pack_partner.2.x_ref, bf16[12288,3072]{1,0:T(8,128)(2,1)} %pack_partner.3.e_ref, bf16[4,1,2048,384]{3,2,1,0:T(8,128)(2,1)} %bitcast.75, bf16[1024,3072]{1,0:T(8,128)(2,1)} %bitcast.74), custom_call_target="tpu_custom_call" | custom-call | flops 180388626432 | bytes 176160768 | tf_op jit(solution)/shard_map/chunk_grads/pallas_call | solution.py:195
  396.3 233.1 %chunk_grads.6 = f32[4,2,1024,768]{3,2,1,0:T(8,128)} custom-call(s32[2]{0:T(128)} %pad_add_fusion.meta, bf16[12288,3072]{1,0:T(8,128)(2,1)} %pack_partner.2.x_ref, bf16[12288,3072]{1,0:T(8,128)(2,1)} %pack_partner.3.e_ref, bf16[4,1,4096,384]{3,2,1,0:T(8,128)(2,1)} %bitcast.70, bf16[4,1,4096,384]{3,2,1,0:T(8,128)(2,1)} %bitcast.71), custom_call_target="tpu_custom_call" | custom-call | flops 180388626432 | bytes 176160768 | tf_op jit(solution)/shard_map/chunk_grads/pallas_call | solution.py:195
  629.8 234.3 %chunk_grads.5 = f32[4,2,1024,768]{3,2,1,0:T(8,128)} custom-call(s32[2]{0:T(128)} %pad_add_fusion.meta, bf16[12288,3072]{1,0:T(8,128)(2,1)} %pack_partner.2.x_ref, bf16[12288,3072]{1,0:T(8,128)(2,1)} %pack_partner.3.e_ref, bf16[4,2,4096,384]{3,2,1,0:T(8,128)(2,1)} %bitcast.66, bf16[4,2,4096,384]{3,2,1,0:T(8,128)(2,1)} %bitcast.67), custom_call_target="tpu_custom_call" | custom-call | flops 180388626432 | bytes 176160768 | tf_op jit(solution)/shard_map/chunk_grads/pallas_call | solution.py:195
  864.5 234.4 %chunk_grads.4 = (f32[4,4096,384]{2,1,0:T(8,128)}, f32[4,1024,384]{2,1,0:T(8,128)}) custom-call(s32[2]{0:T(128)} %pad_add_fusion.meta, bf16[12288,3072]{1,0:T(8,128)(2,1)} %pack_partner.2.x_ref, bf16[12288,3072]{1,0:T(8,128)(2,1)} %pack_partner.3.e_ref, bf16[4,2,4096,384]{3,2,1,0:T(8,128)(2,1)} %bitcast.68, bf16[4,2,4096,384]{3,2,1,0:T(8,128)(2,1)} %bitcast.69), custom_call_target="tpu_custom_call" | custom-call | flops 180388626432 | bytes 176160768 | tf_op jit(solution)/shard_map/chunk_grads/pallas_call | solution.py:195
  1099.0 10.3 collective-permute-done.4
  1109.3 3.1 constant_dynamic-update-slice_fusion
  1112.4 1.9 slice-done
  1114.3 1.2 constant_dynamic-slice_fusion
  1115.7 2.0 slice-done.1
  1117.7 1.3 constant_dynamic-slice_fusion.1
  1119.2 25.8 %reduce-scatter.7.cloned.1.call-done = f32[2048,768]{1,0:T(8,128)} async-done(((f32[8192,768]{1,0:T(8,128)}), f32[2048,768]{1,0:T(8,128)}) %reduce-scatter.7.cloned.1.call-update) | async-done | bytes 6291472 | tf_op jit(solution)/shard_map/reduce_scatter | solution.py:409
  1145.0 1.9 slice-done.2
  1146.9 1.2 constant_dynamic-slice_fusion.2
  1148.2 9.5 shard_map.68
  1157.7 9.7 shard_map.69
  1168.5 9.5 shard_map.70
  1178.1 186.2 %reduce-scatter.5.cloned.1.call-done.reduced = f32[4096,384]{1,0:T(8,128)} async-done(((f32[16384,384]{1,0:T(8,128)}), f32[4096,384]{1,0:T(8,128)}) %reduce-scatter.5.cloned.1.call-update) | async-done | bytes 6291472 | tf_op jit(solution)/shard_map/reduce_scatter | solution.py:409
  1364.3 5.5 shard_map.71
  (71 shorter events, 13.8 us)
Async XLA Ops:
  7.2 155.6 %all-gather.14.cloned.1.call-start = ((), (), s32[]{:S(2)}) async-start(), calls=%async_computation.11 | async-start | bytes 7864320 | tf_op jit(solution)/shard_map/all_gather | solution.py:379
  11.0 151.8 %all-gather.12.cloned.1.call-start = ((), (), s32[]{:S(2)}) async-start(), calls=%async_computation.10 | async-start | bytes 7864320 | tf_op jit(solution)/shard_map/all_gather | solution.py:369
  15.6 8.2 collective-permute-start.3
  21.3 5.1 copy-start.4
  23.8 5.8 copy-start
  26.3 370.0 %all-gather.10.cloned.1.call-start = ((), (), s32[]{:S(2)}) async-start(), calls=%async_computation.9 | async-start | bytes 15728640 | tf_op jit(solution)/shard_map/all_gather | solution.py:369
  26.3 3.5 copy-start.1
  26.4 3.5 copy-start.2
  26.4 1.2 collective-permute-start
  27.6 65.5 %collective-permute-start.2 = (bf16[12,512,3072]{2,1,0:T(8,128)(2,1)}, bf16[12,512,3072]{2,1,0:T(8,128)(2,1)}, u32[]{:S(2)}, u32[]{:S(2)}) collective-permute-start(bf16[12,512,3072]{2,1,0:T(8,128)(2,1)} %in_ref.3), channel_id=1, source_target_pairs={{0,1},{1,0},{2,3},{3,2},{4,5},{5,4},{6,7},{7,6}} | collective-permute-start | bytes 113246216 | tf_op jit(solution)/shard_map/ppermute | solution.py:360
  31.8 1.9 slice-start.3
  31.8 598.0 %all-gather.8.cloned.1.call-start = ((), (), s32[]{:S(2)}) async-start(), calls=%async_computation.4 | async-start | bytes 31457280 | tf_op jit(solution)/shard_map/all_gather | solution.py:369
  31.9 105.2 %collective-permute-start.1 = (bf16[12,512,3072]{2,1,0:T(8,128)(2,1)}, bf16[12,512,3072]{2,1,0:T(8,128)(2,1)}, u32[]{:S(2)}, u32[]{:S(2)}) collective-permute-start(bf16[12,512,3072]{2,1,0:T(8,128)(2,1)} %in_ref.2), channel_id=1, source_target_pairs={{0,1},{1,0},{2,3},{3,2},{4,5},{5,4},{6,7},{7,6}} | collective-permute-start | bytes 113246216 | tf_op jit(solution)/shard_map/ppermute | solution.py:359
  34.7 1.4 slice-start.4
  34.7 1.9 slice-start.5
  39.6 1072.9 %reduce-scatter.11.cloned.1.call-start = ((), (), s32[]{:S(2)}) async-start(), calls=%async_computation.8 | async-start | bytes 31457280 | tf_op jit(solution)/shard_map/reduce_scatter | solution.py:409
  396.0 719.7 %reduce-scatter.9.cloned.1.call-start = ((), (), s32[]{:S(2)}) async-start(), calls=%async_computation.7 | async-start | bytes 31457280 | tf_op jit(solution)/shard_map/reduce_scatter | solution.py:409
  629.5 515.6 %reduce-scatter.7.cloned.1.call-start = ((), (), s32[]{:S(2)}) async-start(), calls=%async_computation.6 | async-start | bytes 31457280 | tf_op jit(solution)/shard_map/reduce_scatter | solution.py:409
  864.1 500.2 %reduce-scatter.5.cloned.1.call-start = ((), (), s32[]{:S(2)}) async-start(), calls=%async_computation.5 | async-start | bytes 31457280 | tf_op jit(solution)/shard_map/reduce_scatter | solution.py:409
  1098.9 10.4 collective-permute-start.4
  1112.4 1.9 slice-start
  1115.6 32.6 %collective-permute-start.7 = (f32[1024,384]{1,0:T(8,128)}, f32[1024,384]{1,0:T(8,128)}, u32[]{:S(2)}, u32[]{:S(2)}) collective-permute-start(f32[1024,384]{1,0:T(8,128)} %constant_dynamic-slice_fusion), channel_id=1, source_target_pairs={{0,1},{1,0},{2,3},{3,2},{4,5},{5,4},{6,7},{7,6}} | collective-permute-start | bytes 4718600 | tf_op jit(solution)/shard_map/ppermute | solution.py:415
  1115.7 2.0 slice-start.1
  1118.9 38.8 %collective-permute-start.6 = (f32[1024,384]{1,0:T(8,128)}, f32[1024,384]{1,0:T(8,128)}, u32[]{:S(2)}, u32[]{:S(2)}) collective-permute-start(f32[1024,384]{1,0:T(8,128)} %constant_dynamic-slice_fusion.1), channel_id=1, source_target_pairs={{0,1},{1,0},{2,3},{3,2},{4,5},{5,4},{6,7},{7,6}} | collective-permute-start | bytes 4718600 | tf_op jit(solution)/shard_map/ppermute | solution.py:415
  1145.0 1.9 slice-start.2
  1148.2 19.2 %collective-permute-start.5 = (f32[1024,384]{1,0:T(8,128)}, f32[1024,384]{1,0:T(8,128)S(1)}, u32[]{:S(2)}, u32[]{:S(2)}) collective-permute-start(f32[1024,384]{1,0:T(8,128)} %constant_dynamic-slice_fusion.2), channel_id=1, source_target_pairs={{0,1},{1,0},{2,3},{3,2},{4,5},{5,4},{6,7},{7,6}} | collective-permute-start | bytes 4718600 | tf_op jit(solution)/shard_map/ppermute | solution.py:415
  1167.4 1.1 copy-start.3
Sparse Core Ops, SparseCore 0:
  11.1 67.2 all-gather.13
  80.2 64.4 all-gather.11
  146.5 116.8 all-gather.9
  265.6 222.0 all-gather.7
  490.5 216.1 reduce-scatter.10
  709.6 216.1 reduce-scatter.8
  928.8 216.1 reduce-scatter.6
  1148.1 216.1 reduce-scatter.4
